TPU v7x, 64 devices: a 2x2x8 block of a 4x4x8 slice. The times are simulated.
64 devices in a mesh: rep: 4 (over x, y), dp: 16 (over z, core).
Axes of the slice: x: 2, y: 2, z: 8, core: 2. Of those that a mesh axis runs over, the one named last changes fastest.
The devices are a block of a 4x4x8 slice.
Arguments:
- x: bfloat16 [64, 2048, 768], P(('rep', 'dp')), parts along dimension 0
- dy: bfloat16 [64, 2048, 768], P(('rep', 'dp')), parts along dimension 0
- w_gate: bfloat16 [2, 768, 1792], replicated
- w_up: bfloat16 [2, 768, 1792], replicated
- w_down: bfloat16 [2, 1792, 768], replicated
- m_w_gate: float32 [2, 768, 1792], replicated
- m_w_up: float32 [2, 768, 1792], replicated
- m_w_down: float32 [2, 1792, 768], replicated
- v_w_gate: float32 [2, 768, 1792], replicated
- v_w_up: float32 [2, 768, 1792], replicated
- v_w_down: float32 [2, 1792, 768], replicated
Outputs:
- output 1: bfloat16 [8, 768, 1792], P('rep'), parts along dimension 0
- output 2: bfloat16 [8, 768, 1792], P('rep'), parts along dimension 0
- output 3: bfloat16 [8, 1792, 768], P('rep'), parts along dimension 0
- output 4: float32 [8, 768, 1792], P('rep'), parts along dimension 0
- output 5: float32 [8, 768, 1792], P('rep'), parts along dimension 0
- output 6: float32 [8, 1792, 768], P('rep'), parts along dimension 0
- output 7: float32 [8, 768, 1792], P('rep'), parts along dimension 0
- output 8: float32 [8, 768, 1792], P('rep'), parts along dimension 0
- output 9: float32 [8, 1792, 768], P('rep'), parts along dimension 0
There are 4 independent parts. A program takes and returns all parts, laid end to end along the dimension named above; an argument that names none is the same for every part.
All inputs are finite; a program needn't handle non-finite values.
Results may differ from a plain program's by a relative error of at most 0.0224.
Values are sent between devices in bfloat16 or wider.
A program may use at most 768 MiB of HBM per device.

v0:
```python
import jax
import jax.numpy as jnp
from jax import lax
from jax.sharding import PartitionSpec as P

NAMES = ("w_gate", "w_up", "w_down")


def matmul(a, w):
    return jnp.dot(a, w, preferred_element_type=jnp.float32).astype(jnp.bfloat16)


def normed(h):
    wide = h.astype(jnp.float32)
    scale = lax.rsqrt(jnp.mean(wide**2, -1, keepdims=True) + 1e-6)
    return (wide * scale).astype(jnp.bfloat16)


def layer(h, w):
    a = normed(h)
    gate = jnp.dot(a, w["w_gate"], preferred_element_type=jnp.float32)
    up = jnp.dot(a, w["w_up"], preferred_element_type=jnp.float32)
    return h + matmul((jax.nn.silu(gate) * up).astype(jnp.bfloat16), w["w_down"])


def adamw(w, m, v, g):
    m = 0.9 * m + 0.1 * g
    v = 0.95 * v + 0.05 * g * g
    step = m * lax.rsqrt(v + 1e-8) + 0.1 * w
    return (w - 0.02 * step).astype(jnp.bfloat16), m, v


def clipped(gradients, sum_of_squares, count):
    factor = jnp.minimum(1.0, 0.5 * lax.rsqrt(sum_of_squares / count + 1e-30))
    return [g * factor for g in gradients]


def solution(mesh):
    def step(x, dy, *arrays):
        weights, m, v = (arrays[i : i + 3] for i in (0, 3, 6))
        layers = weights[0].shape[0]
        h, kept = x[0], []
        for number in range(layers):
            kept.append(h)
            h = layer(h, {name: w[number] for name, w in zip(NAMES, weights, strict=True)})
        by_h, summed = dy[0], [None] * layers
        for number in reversed(range(layers)):
            _, back = jax.vjp(lambda w, h: layer(h, w), {name: w[number] for name, w in zip(NAMES, weights, strict=True)}, kept[number])
            by_w, by_h = back(by_h)
            summed[number] = [lax.psum(by_w[name], "dp") for name in NAMES]
        gradients = [jnp.stack([summed[number][i] for number in range(layers)]).astype(jnp.float32) for i in range(3)]
        gradients = clipped(gradients, sum(jnp.sum(g * g) for g in gradients), sum(g.size for g in gradients))
        new = [adamw(w.astype(jnp.float32), m, v, g) for w, m, v, g in zip(weights, m, v, gradients, strict=True)]
        return tuple(one[which] for which in range(3) for one in new)

    return jax.shard_map(
        step,
        mesh=mesh,
        in_specs=(P(("rep", "dp"), None, None),) * 2 + (P(None, None, None),) * 9,
        out_specs=(P("rep", None, None),) * 9,
        check_vma=False,
    )
```

profile of v0, /device:TPU:21, one launch (start us, length us, event | category | flops | bytes accessed | tf_op | source)
XLA Modules:
  0.0 489.8 jit_solution(14249934390109194212)
XLA Ops:
  7.3 3.2 copy.20
  11.2 5.0 %copy.21 = bf16[1,2048,768]{1,2,0:T(8,128)(2,1)} copy(bf16[1,2048,768]{2,1,0:T(8,128)(2,1)} %param.12) | data formatting | bytes 6291456 | tf_op args[1]
  16.2 10.3 %convolution_convert_fusion.1 = bf16[2048,1792]{1,0:T(8,128)(2,1)} fusion(bf16[1,2048,768]{2,1,0:T(8,128)(2,1)} %param.12, bf16[2,1792,768]{2,1,0:T(8,128)(2,1)} %param.15), kind=kOutput, calls=%fused_computation.66 | convolution fusion | flops 5640814592 | bytes 13238272 | tf_op jit(solution)/shard_map/transpose(jvp())/dot_general | solution.py:10
  26.5 11.1 %fusion.77 = f32[2048,1792]{1,0:T(8,128)} fusion(bf16[2,768,1792]{2,1,0:T(8,128)(2,1)} %param.13, bf16[1,2048,768]{2,1,0:T(8,128)(2,1)S(1)} %copy-done.5, f32[2048]{0:T(1024)S(1)} %add_rsqrt_fusion), kind=kOutput, calls=%fused_computation.111 | convolution fusion | flops 5641863168 | bytes 20586496 | tf_op jit(solution)/shard_map/dot_general | solution.py:21
  37.6 16.2 %multiply_convert_fusion.1 = (bf16[2048,1792]{1,0:T(8,128)(2,1)}, f32[2048,1792]{1,0:T(8,128)}) fusion(f32[2048,1792]{1,0:T(8,128)} %fusion.77, bf16[2,768,1792]{2,1,0:T(8,128)(2,1)S(1)} %bitcast.77, bf16[1,2048,768]{2,1,0:T(8,128)(2,1)} %param.11, f32[2048]{0:T(1024)S(1)} %add_rsqrt_fusion), kind=kOutput, calls=%fused_computation.20 | convolution fusion | flops 5663883264 | bytes 42606592 | tf_op jit(solution)/shard_map/dot_general | solution.py:22
  53.9 9.7 %fusion.40 = (f32[2048]{0:T(1024)S(1)}, bf16[2048,768]{0,1:T(8,128)(2,1)S(1)}) fusion(bf16[2048,1792]{1,0:T(8,128)(2,1)} %get-tuple-element.24, bf16[2,1792,768]{2,1,0:T(8,128)(2,1)} %param.15, bf16[1,2048,768]{1,2,0:T(8,128)(2,1)S(1)} %copy.20), kind=kOutput, calls=%fused_computation.73 | convolution fusion | flops 5645006848 | bytes 16392192 | tf_op jit(solution)/shard_map/dot_general | solution.py:10
  65.2 9.3 %fusion.66 = f32[2048,1792]{1,0:T(8,128)} fusion(bf16[2,768,1792]{2,1,0:T(8,128)(2,1)S(1)} %bitcast.77, bf16[2048,768]{0,1:T(8,128)(2,1)S(1)} %get-tuple-element.27, f32[2048]{0:T(1024)S(1)} %fusion.100), kind=kOutput, calls=%fused_computation.100 | convolution fusion | flops 5641863168 | bytes 20586496 | tf_op jit(solution)/shard_map/jvp()/dot_general | solution.py:22
  74.5 23.3 %fusion.2 = (bf16[2048,1792]{1,0:T(8,128)(2,1)}, f32[2048,1792]{1,0:T(8,128)}) fusion(f32[2048,1792]{1,0:T(8,128)} %fusion.66, bf16[2048,1792]{1,0:T(8,128)(2,1)} %convolution_convert_fusion.1, bf16[2,768,1792]{2,1,0:T(8,128)(2,1)} %param.13, bf16[2048,768]{0,1:T(8,128)(2,1)} %copy-done.7, f32[2048]{0:T(1024)S(1)} %fusion.100), kind=kOutput, calls=%fused_computation.11 | convolution fusion | flops 5685903360 | bytes 49946624 | tf_op jit(solution)/shard_map/jvp()/dot_general | solution.py:21
  97.8 10.8 %fusion.57 = bf16[1,768,1792]{2,1,0:T(8,128)(2,1)} fusion(bf16[2048,1792]{1,0:T(8,128)(2,1)} %get-tuple-element.28, bf16[2048,768]{0,1:T(8,128)(2,1)S(1)} %copy-done.8, f32[2048]{0:T(1024)S(1)} %fusion.100), kind=kOutput, calls=%fused_computation.95 | convolution fusion | flops 5641863168 | bytes 13246464 | tf_op jit(solution)/shard_map/transpose(jvp())/dot_general | solution.py:21
  108.6 9.2 %convolution_convert_fusion.4 = bf16[2048,768]{0,1:T(8,128)(2,1)} fusion(bf16[2048,1792]{1,0:T(8,128)(2,1)S(1)} %copy-done.14, bf16[2,768,1792]{2,1,0:T(8,128)(2,1)} %param.13), kind=kOutput, calls=%fused_computation.82 | convolution fusion | flops 5637144576 | bytes 13238272 | tf_op jit(solution)/shard_map/transpose(jvp())/dot_general | solution.py:21
  117.8 14.1 %fusion.61 = bf16[1,1792,768]{2,1,0:T(8,128)(2,1)} fusion(bf16[1,2048,768]{2,1,0:T(8,128)(2,1)S(1)} %copy-done.6, f32[2048,1792]{1,0:T(8,128)} %fusion.66, f32[2048,1792]{1,0:T(8,128)} %get-tuple-element.29), kind=kOutput, calls=%fused_computation.99 | convolution fusion | flops 5660540928 | bytes 35258368 | tf_op jit(solution)/shard_map/transpose(jvp())/dot_general | solution.py:10
  131.9 12.5 %fusion.60 = bf16[1,768,1792]{2,1,0:T(8,128)(2,1)} fusion(bf16[2048,1792]{1,0:T(8,128)(2,1)} %convolution_convert_fusion.1, bf16[2048,768]{0,1:T(8,128)(2,1)S(1)} %copy-done.9, f32[2048]{0:T(1024)S(1)} %fusion.100, f32[2048,1792]{1,0:T(8,128)} %get-tuple-element.29), kind=kOutput, calls=%fused_computation.98 | convolution fusion | flops 5665259520 | bytes 27926528 | tf_op jit(solution)/shard_map/transpose(jvp())/dot_general | solution.py:22
  144.4 14.0 %fusion.42 = (f32[2048]{0:T(1024)S(1)}, bf16[2048,768]{0,1:T(8,128)(2,1)}) fusion(bf16[2048,768]{0,1:T(8,128)(2,1)} %copy-done.7, bf16[2048,768]{0,1:T(8,128)(2,1)} %convolution_convert_fusion.4, bf16[2,768,1792]{2,1,0:T(8,128)(2,1)S(1)} %bitcast.79, bf16[2048,1792]{1,0:T(8,128)(2,1)} %convolution_convert_fusion.1, f32[2048,1792]{1,0:T(8,128)} %get-tuple-element.29), kind=kOutput, calls=%fused_computation.75 | convolution fusion | flops 5668599808 | bytes 34217984 | tf_op jit(solution)/shard_map/transpose(jvp())/dot_general | solution.py:22
  158.5 5.2 %fusion.51 = bf16[2048,768]{0,1:T(8,128)(2,1)S(1)} fusion(bf16[2048,768]{0,1:T(8,128)(2,1)} %copy-done.7, bf16[2048,768]{0,1:T(8,128)(2,1)} %get-tuple-element.31, bf16[1,2048,768]{1,2,0:T(8,128)(2,1)S(1)} %copy-done.2, f32[2048]{0:T(1024)S(1)} %multiply_multiply_fusion.3, f32[2048]{0:T(1024)S(1)} %fusion.100), kind=kLoop, calls=%fused_computation.90 | loop fusion | flops 11010048 | bytes 12599296 | tf_op jit(solution)/shard_map/transpose(jvp())/add_any | solution.py:14
  163.6 9.4 %fusion.58 = bf16[1,1792,768]{2,1,0:T(8,128)(2,1)} fusion(bf16[2048,1792]{1,0:T(8,128)(2,1)} %get-tuple-element.24, bf16[2048,768]{0,1:T(8,128)(2,1)S(1)} %fusion.51), kind=kOutput, calls=%fused_computation.96 | convolution fusion | flops 5638520832 | bytes 13238272 | tf_op jit(solution)/shard_map/transpose(jvp())/dot_general | solution.py:10
  173.1 6.4 %convolution_convert_fusion = bf16[2048,1792]{1,0:T(8,128)(2,1)S(1)} fusion(bf16[2048,768]{0,1:T(8,128)(2,1)S(1)} %fusion.51, bf16[2,1792,768]{2,1,0:T(8,128)(2,1)S(1)} %bitcast.81), kind=kOutput, calls=%fused_computation.65 | convolution fusion | flops 5640814592 | bytes 13238272 | tf_op jit(solution)/shard_map/transpose(jvp())/dot_general | solution.py:10
  179.5 14.2 %fusion.59 = bf16[1,768,1792]{2,1,0:T(8,128)(2,1)} fusion(bf16[2048,1792]{1,0:T(8,128)(2,1)S(1)} %convolution_convert_fusion, bf16[1,2048,768]{1,2,0:T(8,128)(2,1)S(1)} %copy-done.1, f32[2048]{0:T(1024)S(1)} %copy-done.13, f32[2048,1792]{1,0:T(8,128)} %fusion.77), kind=kOutput, calls=%fused_computation.97 | convolution fusion | flops 5665259520 | bytes 27926528 | tf_op jit(solution)/shard_map/transpose(jvp())/dot_general | solution.py:22
  193.7 17.0 %fusion.54 = bf16[1,768,1792]{2,1,0:T(8,128)(2,1)} fusion(f32[2048,1792]{1,0:T(8,128)} %fusion.77, f32[2048,1792]{1,0:T(8,128)} %get-tuple-element.25, bf16[2048,1792]{1,0:T(8,128)(2,1)} %copy-done.15, bf16[1,2048,768]{1,2,0:T(8,128)(2,1)S(1)} %copy-done.1, f32[2048]{0:T(1024)S(1)} %copy-done.13), kind=kOutput, calls=%fused_computation.94 | convolution fusion | flops 5683609600 | bytes 42606592 | tf_op jit(solution)/shard_map/transpose(jvp())/dot_general | solution.py:21
  210.8 194.7 %all-reduce.3.cloned.1.call-done = (bf16[1,768,1792]{2,1,0:T(8,128)(2,1)}, bf16[1,768,1792]{2,1,0:T(8,128)(2,1)}, bf16[1,768,1792]{2,1,0:T(8,128)(2,1)}, bf16[1,...) async-done(((bf16[1,768,1792]{2,1,0:T(8,128)(2,1)}, bf16[1,768,1792]{2,1,0:T(8,128)(2,1)}, bf16[1,768,1792]{2,1,0:T(8,128)(2,1)}, ...) | async-done | bytes 16515088 | tf_op jit(solution)/shard_map/psum | solution.py:50
  405.5 6.2 %fusion.22 = f32[]{:T(128)} fusion(bf16[1,1792,768]{2,1,0:T(8,128)(2,1)} %get-tuple-element.13, bf16[1,1792,768]{2,1,0:T(8,128)(2,1)} %get-tuple-element.14), kind=kLoop, calls=%fused_computation.46 | loop fusion | flops 11010047 | bytes 5505028 | tf_op jit(solution)/shard_map/reduce_sum | solution.py:52
  411.7 6.0 %fusion.21 = f32[]{:T(128)} fusion(bf16[1,768,1792]{2,1,0:T(8,128)(2,1)} %get-tuple-element.11, bf16[1,768,1792]{2,1,0:T(8,128)(2,1)} %get-tuple-element.12), kind=kLoop, calls=%fused_computation.45 | loop fusion | flops 11010047 | bytes 5505028 | tf_op jit(solution)/shard_map/reduce_sum | solution.py:52
  417.7 3.4 fusion.20
  423.2 21.9 %fusion.28 = (bf16[2,1792,768]{2,1,0:T(8,128)(2,1)}, f32[2,1792,768]{2,1,0:T(8,128)}, f32[2,1792,768]{2,1,0:T(8,128)}) fusion(bf16[2,1792,768]{2,1,0:T(8,128)(2,1)} %param.15, f32[]{:T(128)S(6)} %min_shard_map.3, bf16[1,1792,768]{2,1,0:T(8,128)(2,1)} %get-tuple-element.13, bf16[1,1792,768]{2,1,0:T(8,128)(2,1)} %get-tuple-element.14, ...), kind=kLoop, calls=%fused_computation.52 | loop fusion | flops 55050240 | bytes 60555268 | tf_op jit(solution)/shard_map/convert_element_type | solution.py:30
  445.1 37.3 %fusion.19 = (bf16[2,768,1792]{2,1,0:T(8,128)(2,1)}, f32[2,768,1792]{2,1,0:T(8,128)}, f32[2,768,1792]{2,1,0:T(8,128)}, bf16[2,768,1792]{2,1,0:T(8,128)(2,1)}, f3...) fusion(bf16[2,768,1792]{2,1,0:T(8,128)(2,1)} %param.13, f32[]{:T(128)S(6)} %min_shard_map.3, ...), kind=kLoop, calls=%fused_computation.43 | loop fusion | flops 110100480 | bytes 121110528 | tf_op jit(solution)/shard_map/convert_element_type | solution.py:30
  (53 shorter events, 2.5 us)
Async XLA Ops:
  7.2 398.3 %all-reduce.3.cloned.1.call-start = ((), (), s32[]{:S(2)}) async-start(), calls=%async_computation | async-start | bytes 33030144 | tf_op jit(solution)/shard_map/psum | solution.py:50
  10.5 43.4 %copy-start = (bf16[1,2048,768]{1,2,0:T(8,128)(2,1)}, bf16[1,2048,768]{1,2,0:T(8,128)(2,1)S(1)}, u32[]{:S(2)}) copy-start(bf16[1,2048,768]{1,2,0:T(8,128)(2,1)S(1)} %copy.20) | copy-start | bytes 9437188
  11.1 26.5 %copy-start.12 = (f32[2048]{0:T(1024)}, f32[2048]{0:T(1024)S(1)}, u32[]{:S(2)}) copy-start(f32[2048]{0:T(1024)S(1)} %add_rsqrt_fusion) | copy-start | bytes 24580
  16.2 10.4 %copy-start.5 = (bf16[1,2048,768]{2,1,0:T(8,128)(2,1)S(1)}, bf16[1,2048,768]{2,1,0:T(8,128)(2,1)}, u32[]{:S(2)}) copy-start(bf16[1,2048,768]{2,1,0:T(8,128)(2,1)} %param.11) | copy-start | bytes 9437188
  16.2 21.4 %slice-start = ((s8[5505024]{0:T(1024)(128)(4,1)}), s8[4194304]{0:T(1024)(128)(4,1)S(1)}, s32[]{:S(2)}) async-start(s8[5505024]{0:T(1024)(128)(4,1)} %bitcast.76), calls=%async_computation.1 | async-start | bytes 8388608
  26.5 11.1 %slice-start.1 = ((s8[5505024]{0:T(1024)(128)(4,1)}), s8[1310720]{0:T(1024)(128)(4,1)S(1)}, s32[]{:S(2)}) async-start(s8[5505024]{0:T(1024)(128)(4,1)} %bitcast.76), calls=%async_computation.2 | async-start | bytes 2621440
  63.5 1.7 copy-start.7
  63.6 1.7 copy-start.10
  74.5 23.3 %copy-start.8 = (bf16[2048,768]{0,1:T(8,128)(2,1)S(1)}, bf16[2048,768]{0,1:T(8,128)(2,1)}, u32[]{:S(2)}) copy-start(bf16[2048,768]{0,1:T(8,128)(2,1)} %copy-done.7) | copy-start | bytes 9437188
  97.8 10.8 %copy-start.14 = (bf16[2048,1792]{1,0:T(8,128)(2,1)S(1)}, bf16[2048,1792]{1,0:T(8,128)(2,1)}, u32[]{:S(2)}) copy-start(bf16[2048,1792]{1,0:T(8,128)(2,1)} %get-tuple-element.28) | copy-start | bytes 22020100
  108.6 9.2 %copy-start.6 = (bf16[1,2048,768]{2,1,0:T(8,128)(2,1)S(1)}, bf16[1,2048,768]{2,1,0:T(8,128)(2,1)}, u32[]{:S(2)}) copy-start(bf16[1,2048,768]{2,1,0:T(8,128)(2,1)} %param.12) | copy-start | bytes 9437188
  117.8 14.1 %copy-start.9 = (bf16[2048,768]{0,1:T(8,128)(2,1)S(1)}, bf16[2048,768]{0,1:T(8,128)(2,1)}, u32[]{:S(2)}) copy-start(bf16[2048,768]{0,1:T(8,128)(2,1)} %copy-done.7) | copy-start | bytes 9437188
  117.8 26.6 %slice-start.2 = ((s8[5505024]{0:T(1024)(128)(4,1)}), s8[4194304]{0:T(1024)(128)(4,1)S(1)}, s32[]{:S(2)}) async-start(s8[5505024]{0:T(1024)(128)(4,1)} %bitcast.78), calls=%async_computation.3 | async-start | bytes 8388608
  131.9 12.5 %slice-start.3 = ((s8[5505024]{0:T(1024)(128)(4,1)}), s8[1310720]{0:T(1024)(128)(4,1)S(1)}, s32[]{:S(2)}) async-start(s8[5505024]{0:T(1024)(128)(4,1)} %bitcast.78), calls=%async_computation.4 | async-start | bytes 2621440
  144.4 14.0 %copy-start.11 = (f32[2048]{0:T(1024)S(1)}, f32[2048]{0:T(1024)}, u32[]{:S(2)}) copy-start(f32[2048]{0:T(1024)} %copy-done.10) | copy-start | bytes 24580
  144.4 14.0 %copy-start.2 = (bf16[1,2048,768]{1,2,0:T(8,128)(2,1)S(1)}, bf16[1,2048,768]{1,2,0:T(8,128)(2,1)}, u32[]{:S(2)}) copy-start(bf16[1,2048,768]{1,2,0:T(8,128)(2,1)} %copy.21) | copy-start | bytes 9437188
  158.5 14.6 %slice-start.4 = ((s8[5505024]{0:T(1024)(128)(4,1)}), s8[1310720]{0:T(1024)(128)(4,1)S(1)}, s32[]{:S(2)}) async-start(s8[5505024]{0:T(1024)(128)(4,1)} %bitcast.80), calls=%async_computation.5 | async-start | bytes 2621440
  163.6 9.4 %slice-start.5 = ((s8[5505024]{0:T(1024)(128)(4,1)}), s8[4194304]{0:T(1024)(128)(4,1)S(1)}, s32[]{:S(2)}) async-start(s8[5505024]{0:T(1024)(128)(4,1)} %bitcast.80), calls=%async_computation.6 | async-start | bytes 8388608
  173.1 6.4 %copy-start.1 = (bf16[1,2048,768]{1,2,0:T(8,128)(2,1)S(1)}, bf16[1,2048,768]{1,2,0:T(8,128)(2,1)}, u32[]{:S(2)}) copy-start(bf16[1,2048,768]{1,2,0:T(8,128)(2,1)} %copy-done) | copy-start | bytes 9437188
  173.1 6.4 %copy-start.13 = (f32[2048]{0:T(1024)S(1)}, f32[2048]{0:T(1024)}, u32[]{:S(2)}) copy-start(f32[2048]{0:T(1024)} %copy-done.12) | copy-start | bytes 24580
  179.5 14.2 %copy-start.15 = (bf16[2048,1792]{1,0:T(8,128)(2,1)}, bf16[2048,1792]{1,0:T(8,128)(2,1)S(1)}, u32[]{:S(2)}) copy-start(bf16[2048,1792]{1,0:T(8,128)(2,1)S(1)} %convolution_convert_fusion) | copy-start | bytes 22020100
  405.5 12.2 %copy-start.3 = (bf16[1,768,1792]{2,1,0:T(8,128)(2,1)S(1)}, bf16[1,768,1792]{2,1,0:T(8,128)(2,1)}, u32[]{:S(2)}) copy-start(bf16[1,768,1792]{2,1,0:T(8,128)(2,1)} %get-tuple-element.9) | copy-start | bytes 8257540
  405.5 12.2 %copy-start.4 = (bf16[1,768,1792]{2,1,0:T(8,128)(2,1)S(1)}, bf16[1,768,1792]{2,1,0:T(8,128)(2,1)}, u32[]{:S(2)}) copy-start(bf16[1,768,1792]{2,1,0:T(8,128)(2,1)} %get-tuple-element.10) | copy-start | bytes 8257540
Sparse Core Ops, SparseCore 0:
  210.9 194.5 all-reduce.2
where the time goes:
time: 497 us; the launch traced here: 490 us
  waiting for transfers between devices  195 us (39%)
  matrix products  187 us (38%)
  other arithmetic  80.7 us (16%)
  between operations  16.8 us (3%)
  local copies, waits for them, and re-layouts  9.95 us (2%)
    psum x1, waiting for transfers between devices, step(): summed[number] = [lax.psum(by_w[name], 'dp') for name in NAMES]  195 us
    dot_general x5, matrix products, layer(): gate = jnp.dot(a, w['w_gate'], preferred_element_type=jnp.float32)  71.4 us
    dot_general x5, matrix products, layer(): up = jnp.dot(a, w['w_up'], preferred_element_type=jnp.float32)  66.1 us
    convert_element_type x2, other arithmetic, adamw(): return ((w - 0.02 * step).astype(jnp.bfloat16), m, v)  59.2 us
    dot_general x5, matrix products, matmul(): jnp.dot(a, w, preferred_element_type=jnp.float32).astype(jnp.bfloat16)  50 us
    reduce_sum x3, other arithmetic, step(): jnp.sum(g * g)  15.7 us
    unnamed x46, local copies, waits for them, and re-layouts  9.95 us
  transfers between devices with their start and end apart: 1, of which 1 were waited for; matrix products, arithmetic and copies ran while one was open for 0% of the time, Pallas kernels for 0%

commit v1 on v0

v1 whole, which is shorter than its diff:
```python
import functools

import jax
import jax.numpy as jnp
from jax import lax
from jax.experimental import pallas as pl
from jax.experimental.pallas import tpu as pltpu
from jax.sharding import PartitionSpec as P

BLOCK = 256
ROWS = 512
VMEM = 64 * 1024 * 1024 - 65536
F32, BF16 = jnp.float32, jnp.bfloat16


def dot(a, b):
    return jnp.dot(a, b, preferred_element_type=F32)


def sigmoid(x):
    return 0.5 * jnp.tanh(0.5 * x) + 0.5


def inverse_rms(wide):
    return lax.rsqrt(jnp.mean(wide * wide, -1, keepdims=True) + 1e-6)


def normed(h):
    wide = h.astype(F32)
    return (wide * inverse_rms(wide)).astype(BF16)


def row_loop(tokens, body):
    def step(i, _):
        body(pl.ds(pl.multiple_of(i * ROWS, ROWS), ROWS))
        return 0

    lax.fori_loop(0, tokens // ROWS, step, 0)


def forward_kernel(x, gate, up, down, out, a, total):
    tokens = x.shape[0]
    j = pl.program_id(0)

    @pl.when(j == 0)
    def _():
        def start(rows):
            a[rows, :] = normed(x[rows, :])
            total[rows, :] = jnp.zeros((ROWS, total.shape[1]), F32)

        row_loop(tokens, start)

    def rows_of(rows):
        g = dot(a[rows, :], gate[0])
        u = dot(a[rows, :], up[0])
        hidden = (g * sigmoid(g) * u).astype(BF16)
        total[rows, :] += dot(hidden, down[0])

    row_loop(tokens, rows_of)

    @pl.when(j == pl.num_programs(0) - 1)
    def _():
        def finish(rows):
            out[rows, :] = x[rows, :] + total[rows, :].astype(BF16)

        row_loop(tokens, finish)


def block_specs(layer, d):
    return [
        pl.BlockSpec((1, d, BLOCK), lambda j: (layer, 0, j)),
        pl.BlockSpec((1, d, BLOCK), lambda j: (layer, 0, j)),
        pl.BlockSpec((1, BLOCK, d), lambda j: (layer, j, 0)),
    ]


def forward(x, w_gate, w_up, w_down):
    tokens, d = x.shape
    blocks = w_gate.shape[2] // BLOCK
    whole = pl.BlockSpec((tokens, d), lambda j: (0, 0))
    return pl.pallas_call(
        forward_kernel,
        out_shape=jax.ShapeDtypeStruct((tokens, d), BF16),
        grid=(blocks,),
        in_specs=[whole] + block_specs(0, d),
        out_specs=whole,
        scratch_shapes=[pltpu.VMEM((tokens, d), BF16), pltpu.VMEM((tokens, d), F32)],
        compiler_params=pltpu.CompilerParams(vmem_limit_bytes=VMEM),
        name="forward",
    )(x, w_gate, w_up, w_down)


def backward_kernel(last, h, dy, gate, up, down, grads, *rest):
    if last:
        a, a_t, dy_t, both, hidden, down_t = rest
    else:
        dh, a, a_t, dy_t, both, hidden, down_t, w_t, total = rest
    tokens, d = h.shape
    j = pl.program_id(0)

    @pl.when(j == 0)
    def _():
        def start(rows):
            fresh = normed(h[rows, :])
            a[rows, :] = fresh
            a_t[:, rows] = fresh.T
            dy_t[:, rows] = dy[rows, :].T
            if not last:
                total[rows, :] = jnp.zeros((ROWS, d), F32)

        row_loop(tokens, start)

    down_t[...] = down[0].T
    if not last:
        w_t[0:BLOCK, :] = gate[0].T
        w_t[BLOCK:, :] = up[0].T

    def rows_of(rows):
        g = dot(a[rows, :], gate[0])
        u = dot(a[rows, :], up[0])
        dhid = dot(dy[rows, :], down_t[...]).astype(BF16).astype(F32)
        s = sigmoid(g)
        act = g * s
        hidden[rows, :] = (act * u).astype(BF16)
        both[rows, 0:BLOCK] = (dhid * u * (s + act * (1.0 - s))).astype(BF16)
        both[rows, BLOCK:] = (dhid * act).astype(BF16)
        if not last:
            total[rows, :] += dot(both[rows, :], w_t[...])

    row_loop(tokens, rows_of)
    grads[0, 0:d, :] = dot(a_t[...], both[:, 0:BLOCK]).astype(BF16)
    grads[0, d : 2 * d, :] = dot(a_t[...], both[:, BLOCK:]).astype(BF16)
    by_down = dot(dy_t[...], hidden[...])
    for t in range(d // BLOCK):
        grads[0, 2 * d + t * BLOCK : 2 * d + (t + 1) * BLOCK, :] = by_down[t * BLOCK : (t + 1) * BLOCK, :].T.astype(BF16)

    if not last:

        @pl.when(j == pl.num_programs(0) - 1)
        def _():
            def finish(rows):
                wide = h[rows, :].astype(F32)
                scale = inverse_rms(wide)
                by_a = total[rows, :].astype(BF16).astype(F32)
                by_scale = jnp.sum(by_a * wide, -1, keepdims=True)
                by_h = by_a * scale - wide * (scale * scale * scale * by_scale / d)
                dh[rows, :] = dy[rows, :] + by_h.astype(BF16)

            row_loop(tokens, finish)


def backward(layer, last, h, dy, w_gate, w_up, w_down):
    tokens, d = h.shape
    blocks = w_gate.shape[2] // BLOCK
    whole = pl.BlockSpec((tokens, d), lambda j: (0, 0))
    out_shape = [jax.ShapeDtypeStruct((blocks, 3 * d, BLOCK), BF16)]
    out_specs = [pl.BlockSpec((1, 3 * d, BLOCK), lambda j: (j, 0, 0))]
    scratch = [
        pltpu.VMEM((tokens, d), BF16),
        pltpu.VMEM((d, tokens), BF16),
        pltpu.VMEM((d, tokens), BF16),
        pltpu.VMEM((tokens, 2 * BLOCK), BF16),
        pltpu.VMEM((tokens, BLOCK), BF16),
        pltpu.VMEM((d, BLOCK), BF16),
    ]
    if not last:
        out_shape.append(jax.ShapeDtypeStruct((tokens, d), BF16))
        out_specs.append(whole)
        scratch += [pltpu.VMEM((2 * BLOCK, d), BF16), pltpu.VMEM((tokens, d), F32)]
    return pl.pallas_call(
        functools.partial(backward_kernel, last),
        out_shape=out_shape,
        grid=(blocks,),
        in_specs=[whole, whole] + block_specs(layer, d),
        out_specs=out_specs,
        scratch_shapes=scratch,
        compiler_params=pltpu.CompilerParams(vmem_limit_bytes=VMEM),
        name=f"backward_{layer}",
    )(h, dy, w_gate, w_up, w_down)


MESH = pl.DeviceIdType.MESH
LANES = 128
STREAMS = ((0, 4), (4, 3))


def put(grads, block, row, value):
    height = grads.shape[3]
    done = 0
    while done < value.shape[0]:
        piece, at = divmod(row + done, height)
        size = min(height - at, value.shape[0] - done)
        grads[block, piece // 2, piece % 2, at : at + size, :] = value[done : done + size, :]
        done += size


def exchange_kernel(group, h, dy, gate, up, down, other, out, norm_out, *scratch):
    (a, a_t, dy_t, both, hidden, down_t, own_grads, loc, sib0, sib1, ring00, ring01, ring10, ring11, final0, final1, norm, *sems) = scratch
    sib_send, sib_recv, loc_sem, rs_send, rs_recv, ag_send, ag_recv, pass_send, pass_recv, fin_sem, fin_send, fin_recv, norm_send, norm_recv = sems
    ring = ((ring00, ring01), (ring10, ring11))
    sib, final = (sib0, sib1), (final0, final1)
    tokens, d = h.shape
    blocks = own_grads.shape[0]
    chips = group // 2
    j = pl.program_id(0)
    me = lax.axis_index("dp")
    z, c = lax.div(me, 2), lax.rem(me, 2)
    sibling = me + 1 - 2 * c
    ahead = (lax.rem(z + 1, chips) * 2 + c, lax.rem(z + chips - 1, chips) * 2 + c)

    def wrapped(q):
        return lax.rem(q + 2 * chips, chips)

    def remote(src, dst, send, recv, to):
        return pltpu.make_async_remote_copy(
            src_ref=src, dst_ref=dst, send_sem=send, recv_sem=recv, device_id={"dp": to}, device_id_type=MESH
        )

    def sib_copy(layer, block):
        src = other.at[block, :, 1 - c] if layer else own_grads.at[block, :, 1 - c]
        return remote(src, sib[layer].at[block], sib_send.at[layer, block], sib_recv.at[layer, block], sibling)

    def loc_copy(block):
        return pltpu.make_async_copy(other.at[block, :, c], loc.at[block], loc_sem.at[block])

    def rs_copy(layer, s, way, k):
        slots = ring[layer][s]
        return remote(slots.at[way, k], slots.at[way, k + 1], rs_send.at[layer, s, way, k], rs_recv.at[layer, s, way, k], ahead[way])

    def terms(layer, block, q, way):
        lanes = slice(way * LANES, (way + 1) * LANES)
        mine = loc[block, q, :, lanes] if layer else own_grads[block, q, c, :, lanes]
        return mine.astype(F32) + sib[layer][block, q, :, lanes].astype(F32)

    def rs_chunk(way, k):
        return wrapped(z - 1 - k if way == 0 else z + 1 + k)

    def rs_first(layer, s):
        first, count = STREAMS[s]
        for block in range(first, first + count):
            sib_copy(layer, block).wait_recv()
            if layer:
                loc_copy(block).wait()
        for way in range(2):
            for i in range(count):
                ring[layer][s][way, 0, i] = terms(layer, first + i, rs_chunk(way, 0), way).astype(BF16)
            rs_copy(layer, s, way, 0).start()

    def rs_step(layer, s, k):
        first, count = STREAMS[s]
        for way in range(2):
            rs_copy(layer, s, way, k - 1).wait_recv()
            for i in range(count):
                so_far = ring[layer][s][way, k, i].astype(F32)
                ring[layer][s][way, k, i] = (so_far + terms(layer, first + i, rs_chunk(way, k), way)).astype(BF16)
            rs_copy(layer, s, way, k).start()

    def rs_last(layer, s):
        first, count = STREAMS[s]
        total = jnp.zeros((1, LANES), F32)
        for way in range(2):
            rs_copy(layer, s, way, chips - 2).wait_recv()
            for i in range(count):
                so_far = ring[layer][s][way, chips - 1, i].astype(F32)
                summed = (so_far + terms(layer, first + i, z, way)).astype(BF16)
                final[layer][first + i, :, way * LANES : (way + 1) * LANES] = summed
                total += jnp.sum(summed.astype(F32) ** 2, 0, keepdims=True)
        return total

    def place(layer, s, q, core, way):
        first, count = STREAMS[s]
        return out.at[pl.ds(layer * blocks + first, count), q, core, :, pl.ds(way * LANES, LANES)]

    def ag_copy(layer, s, way, k, src=None):
        q = wrapped(z - k if way == 0 else z + k)
        here = place(layer, s, q, c, way)
        return remote(here if src is None else src, here, ag_send.at[layer, s, way, k], ag_recv.at[layer, s, way, k], ahead[way])

    def ag_first_copy(layer, s, way):
        first, count = STREAMS[s]
        return ag_copy(layer, s, way, 0, final[layer].at[pl.ds(first, count), :, pl.ds(way * LANES, LANES)])

    def pass_copy(layer, s, way, k):
        here = place(layer, s, wrapped(z - k if way == 0 else z + k), c, way)
        return remote(here, here, pass_send.at[layer, s, way, k - 1], pass_recv.at[layer, s, way, k - 1], sibling)

    def fin_copies(layer):
        here = out.at[pl.ds(layer * blocks, blocks), z, c]
        return (
            pltpu.make_async_copy(final[layer], here, fin_sem.at[layer]),
            remote(final[layer], here, fin_send.at[layer], fin_recv.at[layer], sibling),
        )

    def ag_first(layer):
        for s in range(2):
            for way in range(2):
                ag_first_copy(layer, s, way).start()
        for copy in fin_copies(layer):
            copy.start()

    def ag_step(layer, s, k, go_on):
        for way in range(2):
            ag_copy(layer, s, way, k - 1).wait_recv()
            if go_on:
                ag_copy(layer, s, way, k).start()
            pass_copy(layer, s, way, k).start()

    def norm_copy(k):
        return remote(norm.at[me], norm.at[me], norm_send.at[k], norm_recv.at[k], lax.rem(me + k, group))

    @pl.when(j == 0)
    def _():
        barrier = pltpu.get_barrier_semaphore()

        def greet(k, _):
            pl.semaphore_signal(barrier, inc=1, device_id={"dp": lax.rem(me + k, group)}, device_id_type=MESH)
            return 0

        lax.fori_loop(1, group, greet, 0)
        pl.semaphore_wait(barrier, group - 1)
        for block in range(blocks):
            sib_copy(1, block).start()
            loc_copy(block).start()

        def start(rows):
            fresh = normed(h[rows, :])
            a[rows, :] = fresh
            a_t[:, rows] = fresh.T
            dy_t[:, rows] = dy[rows, :].T

        row_loop(tokens, start)
        rs_first(1, 0)

    @pl.when(j > 0)
    def _():
        rs_step(1, 0, j)

    down_t[...] = down[0].T

    def rows_of(rows):
        g = dot(a[rows, :], gate[0])
        u = dot(a[rows, :], up[0])
        dhid = dot(dy[rows, :], down_t[...]).astype(BF16).astype(F32)
        s = sigmoid(g)
        act = g * s
        hidden[rows, :] = (act * u).astype(BF16)
        both[rows, 0:BLOCK] = (dhid * u * (s + act * (1.0 - s))).astype(BF16)
        both[rows, BLOCK:] = (dhid * act).astype(BF16)

    row_loop(tokens, rows_of)

    @pl.when(j == 0)
    def _():
        rs_first(1, 1)

    @pl.when(j > 0)
    def _():
        rs_step(1, 1, j)

    put(own_grads, j, 0, dot(a_t[...], both[:, 0:BLOCK]).astype(BF16))
    put(own_grads, j, d, dot(a_t[...], both[:, BLOCK:]).astype(BF16))
    by_down = dot(dy_t[...], hidden[...])
    for t in range(d // BLOCK):
        put(own_grads, j, 2 * d + t * BLOCK, by_down[t * BLOCK : (t + 1) * BLOCK, :].T.astype(BF16))
    sib_copy(0, j).start()

    @pl.when(j == blocks - 1)
    def _():
        rs_first(0, 0)
        squares = rs_last(1, 0)
        rs_first(0, 1)
        squares += rs_last(1, 1)
        ag_first(1)

        def both_rings(k, _):
            for s in range(2):
                rs_step(0, s, k)
                ag_step(1, s, k, True)
            return 0

        lax.fori_loop(1, chips - 1, both_rings, 0)
        squares += rs_last(0, 0)
        squares += rs_last(0, 1)
        ag_first(0)
        norm[me] = jnp.broadcast_to(jnp.sum(squares, -1, keepdims=True), norm.shape[1:])

        def send_norm(k, _):
            norm_copy(k).start()
            return 0

        lax.fori_loop(1, group, send_norm, 0)
        for s in range(2):
            ag_step(1, s, chips - 1, False)

        def last_ring(k, _):
            for s in range(2):
                ag_step(0, s, k, True)
            return 0

        lax.fori_loop(1, chips - 1, last_ring, 0)
        for s in range(2):
            ag_step(0, s, chips - 1, False)

        def wait_norm(k, _):
            copy = norm_copy(k)
            copy.wait_send()
            remote(norm.at[lax.rem(me + group - k, group)], norm.at[lax.rem(me + group - k, group)], norm_send.at[k], norm_recv.at[k], sibling).wait_recv()
            return 0

        lax.fori_loop(1, group, wait_norm, 0)
        norm_out[...] = jnp.sum(norm[...], 0)

        for layer in range(2):

            def wait_sib(block, _, layer=layer):
                sib_copy(layer, block).wait_send()
                return 0

            lax.fori_loop(0, blocks, wait_sib, 0)
            keep, passed = fin_copies(layer)
            keep.wait()
            passed.wait_send()
            other_final = out.at[pl.ds(layer * blocks, blocks), z, 1 - c]
            remote(final[layer], other_final, fin_send.at[layer], fin_recv.at[layer], sibling).wait_recv()

            def wait_rings(k, _, layer=layer):
                for s in range(2):
                    for way in range(2):
                        rs_copy(layer, s, way, k).wait_send()
                        ag_copy(layer, s, way, k).wait_send()
                        passed = pass_copy(layer, s, way, k + 1)
                        passed.wait_send()
                        there = place(layer, s, wrapped(z - k - 1 if way == 0 else z + k + 1), 1 - c, way)
                        remote(there, there, pass_send.at[layer, s, way, k], pass_recv.at[layer, s, way, k], sibling).wait_recv()
                return 0

            lax.fori_loop(0, chips - 1, wait_rings, 0)


def exchange(group, h, dy, w_gate, w_up, w_down, other):
    tokens, d = h.shape
    blocks, chips = w_gate.shape[2] // BLOCK, group // 2
    height = 3 * d // group
    whole = pl.BlockSpec((tokens, d), lambda j: (0, 0), pipeline_mode=pl.Buffered(1))
    half = (blocks, chips, height, BLOCK)
    steps = chips - 1
    rings = [pltpu.VMEM((2, chips, count, height, LANES), BF16) for _, count in STREAMS]
    dma = pltpu.SemaphoreType.DMA
    return pl.pallas_call(
        functools.partial(exchange_kernel, group),
        out_shape=[
            jax.ShapeDtypeStruct((2 * blocks, chips, 2, height, BLOCK), BF16),
            jax.ShapeDtypeStruct((8, LANES), F32),
        ],
        grid=(blocks,),
        in_specs=[whole, whole] + block_specs(0, d) + [pl.BlockSpec(memory_space=pl.ANY)],
        out_specs=[pl.BlockSpec(memory_space=pl.ANY), pl.BlockSpec((8, LANES), lambda j: (0, 0))],
        scratch_shapes=[
            pltpu.VMEM((tokens, d), BF16),
            pltpu.VMEM((d, tokens), BF16),
            pltpu.VMEM((d, tokens), BF16),
            pltpu.VMEM((tokens, 2 * BLOCK), BF16),
            pltpu.VMEM((tokens, BLOCK), BF16),
            pltpu.VMEM((d, BLOCK), BF16),
            pltpu.VMEM((blocks, chips, 2, height, BLOCK), BF16),
            pltpu.VMEM(half, BF16),
            pltpu.VMEM(half, BF16),
            pltpu.VMEM(half, BF16),
            *rings,
            *rings,
            pltpu.VMEM((blocks, height, BLOCK), BF16),
            pltpu.VMEM((blocks, height, BLOCK), BF16),
            pltpu.VMEM((group, 8, LANES), F32),
            dma((2, blocks)),
            dma((2, blocks)),
            dma((blocks,)),
            dma((2, 2, 2, steps)),
            dma((2, 2, 2, steps)),
            dma((2, 2, 2, steps)),
            dma((2, 2, 2, steps)),
            dma((2, 2, 2, steps)),
            dma((2, 2, 2, steps)),
            dma((2,)),
            dma((2,)),
            dma((2,)),
            dma((group,)),
            dma((group,)),
        ],
        compiler_params=pltpu.CompilerParams(vmem_limit_bytes=VMEM, collective_id=0, has_side_effects=True),
        name="exchange",
    )(h, dy, w_gate, w_up, w_down, other)


def adamw_kernel(parts, d, factor, g, *refs):
    ws, ms, vs, new_ws, new_ms, new_vs = (refs[i : i + 3] for i in range(0, 18, 3))
    f = factor[0]

    def update(i, at, grad):
        grad = grad.astype(F32) * f
        m = 0.9 * ms[i][at] + 0.1 * grad
        v = 0.95 * vs[i][at] + 0.05 * grad * grad
        w = ws[i][at].astype(F32)
        new_ws[i][at] = (w - 0.02 * (m * lax.rsqrt(v + 1e-8) + 0.1 * w)).astype(BF16)
        new_ms[i][at] = m
        new_vs[i][at] = v

    def grad_rows(start):
        return g[0, start : start + BLOCK, :]

    for i in range(2):
        for t in range(d // BLOCK):
            update(i, (0, slice(t * BLOCK, (t + 1) * BLOCK), slice(None)), grad_rows(i * d + t * BLOCK))
    for t in range(d // BLOCK):
        update(2, (0, slice(None), slice(t * BLOCK, (t + 1) * BLOCK)), grad_rows(2 * d + t * BLOCK))


def adamw(factor, g, weights, m, v):
    layers, d, ff = weights[0].shape
    blocks = ff // BLOCK
    tall = pl.BlockSpec((1, d, BLOCK), lambda l, j: (l, 0, j))
    flat = pl.BlockSpec((1, BLOCK, d), lambda l, j: (l, j, 0))
    three = [tall, tall, flat]
    return pl.pallas_call(
        functools.partial(adamw_kernel, 1, d),
        out_shape=[jax.ShapeDtypeStruct(o.shape, o.dtype) for o in (*weights, *m, *v)],
        grid=(layers, blocks),
        in_specs=[pl.BlockSpec(memory_space=pltpu.SMEM), pl.BlockSpec((1, 3 * d, BLOCK), lambda l, j: (l * blocks + j, 0, 0))] + three * 3,
        out_specs=three * 3,
        compiler_params=pltpu.CompilerParams(vmem_limit_bytes=VMEM),
        name="adamw",
    )(factor, g, *weights, *m, *v)


def solution(mesh):
    group = mesh.shape["dp"]

    def step(x, dy, *arrays):
        weights, m, v = (arrays[i : i + 3] for i in (0, 3, 6))
        h = forward(x[0], *weights)
        g1, dh = backward(1, False, h, dy[0], *weights)
        blocks, rows, lanes = g1.shape
        g, squares = exchange(group, x[0], dh, *weights, g1.reshape(blocks, group // 2, 2, rows // group, lanes))
        g = g.reshape(2 * blocks, rows, lanes)
        factor = jnp.minimum(1.0, 0.5 * lax.rsqrt(squares[0, :1] / g.size + 1e-30))
        return tuple(adamw(factor, g, weights, m, v))

    return jax.shard_map(
        step,
        mesh=mesh,
        in_specs=(P(("rep", "dp"), None, None),) * 2 + (P(None, None, None),) * 9,
        out_specs=(P("rep", None, None),) * 9,
        check_vma=False,
    )
```

time: 497 us -> 355 us (0.71); the launches traced: 490 us -> 355 us
  Pallas kernels: 0 us -> 352 us
  waiting for transfers between devices: 195 us -> 0 us
  matrix products: 187 us -> 0 us
  other arithmetic: 80.7 us -> 0 us
  between operations: 16.8 us -> 1.5 us
  local copies, waits for them, and re-layouts: 9.95 us -> 1.19 us
    pallas_call x0 -> x4, Pallas kernels: none -> 352 us  [the longest x1 187 us: exchange(): pl.pallas_call(functools.partial(exchange_kernel, group), out_shape=[jax....]
    psum x1 -> x0, waiting for transfers between devices: 195 us -> none  [step(): summed[number] = [lax.psum(by_w[name], 'dp') for name in NAMES]]
    dot_general x15 -> x0, matrix products: 187 us -> none  [the longest x5 71.4 us: layer(): gate = jnp.dot(a, w['w_gate'], preferred_element_type=jnp.float32)]
    convert_element_type x2 -> x0, other arithmetic: 59.2 us -> none  [adamw(): return ((w - 0.02 * step).astype(jnp.bfloat16), m, v)]
    reduce_sum x4 -> x0, other arithmetic: 16.3 us -> none  [the longest x3 15.7 us: step(): jnp.sum(g * g)]
    unnamed x46 -> x0, local copies, waits for them, and re-layouts: 9.95 us -> none
    add_any x1 -> x0, other arithmetic: 5.15 us -> none  [normed(): wide = h.astype(jnp.float32)]
  transfers between devices with their start and end apart: 1 -> 0, of which waited for: 1 -> 0; matrix products, arithmetic and copies ran while one was open for 0% -> 0% of each run, Pallas kernels for 0% -> 0%
where the time goes in v1:
time: 355 us
  Pallas kernels  352 us (99%)
    pallas_call x1, Pallas kernels, exchange(): pl.pallas_call(functools.partial(exchange_kernel, group), out_shape=[jax....  187 us
    pallas_call x1, Pallas kernels, backward(): pl.pallas_call(functools.partial(backward_kernel, last), out_shape=out_sh...  73.1 us
    pallas_call x1, Pallas kernels, adamw(): pl.pallas_call(functools.partial(adamw_kernel, 1, d), out_shape=[jax.Shap...  60.3 us
    pallas_call x1, Pallas kernels, forward(): pl.pallas_call(forward_kernel, out_shape=jax.ShapeDtypeStruct((tokens, d)...  31.3 us

profile of v1, /device:TPU:21, one launch (start us, length us, event | category | flops | bytes accessed | tf_op | source)
XLA Modules:
  0.0 354.8 jit_solution(4634912285347395514)
XLA Ops:
  0.6 31.3 %forward.1.h = bf16[2048,768]{1,0:T(8,128)(2,1)} custom-call(bf16[2048,768]{1,0:T(8,128)(2,1)} %bitcast.6, bf16[2,768,1792]{2,1,0:T(8,128)(2,1)} %refs_0_.1, bf16[2,768,1792]{2,1,0:T(8,128)(2,1)} %refs_1_.1, bf16[2,1792,768]{2,1,0:T(8,128)(2,1)} %refs_2_.1), custom_call_target="tpu_custom_call" | custom-call | tf_op jit(solution)/shard_map/forward/pallas_call | solution.py:81
  32.0 73.1 %backward_1.1 = (bf16[7,2304,256]{2,1,0:T(8,128)(2,1)}, bf16[2048,768]{1,0:T(8,128)(2,1)}) custom-call(bf16[2048,768]{1,0:T(8,128)(2,1)} %forward.1.h, bf16[2048,768]{1,0:T(8,128)(2,1)} %bitcast.9, bf16[2,768,1792]{2,1,0:T(8,128)(2,1)} %refs_0_.1, bf16[2,768,1792]{2,1,0:T(8,128)(2,1)} %refs_1_.1, bf16[2,1792,768]{2,1,0:T(8,128)(2,1)} %refs_2_.1), custom_call_target="tpu_custom_call" | custom-call | tf_op jit(solution)/shard_map/backward_1/pallas_call | solution.py:170
  105.1 187.4 %exchange.1 = (bf16[14,8,2,144,256]{4,3,2,1,0:T(8,128)(2,1)}, f32[8,128]{1,0:T(8,128)}) custom-call(bf16[2048,768]{1,0:T(8,128)(2,1)} %bitcast.7, bf16[2048,768]{1,0:T(8,128)(2,1)} %get-tuple-element.13.dy, bf16[2,768,1792]{2,1,0:T(8,128)(2,1)} %refs_0_.1, bf16[2,768,1792]{2,1,0:T(8,128)(2,1)} %refs_1_.1, bf16[2,1792,768]{2,1,0:T(8,128)(2,1)} %refs_2_.1, ...), custom_call_target="tpu_custom_call" | custom-call | tf_op jit(solution)/shard_map/exchange/pallas_call | solution.py:449
  292.4 1.2 slice.3
  294.3 60.3 %adamw.1 = (bf16[2,768,1792]{2,1,0:T(8,128)(2,1)}, bf16[2,768,1792]{2,1,0:T(8,128)(2,1)}, bf16[2,1792,768]{2,1,0:T(8,128)(2,1)}, f32[2,768,1792]{2,1,0:T(8,128)}...) custom-call(f32[1]{0:T(128)} %bitcast.3.factor, ...), custom_call_target="tpu_custom_call" | custom-call | tf_op jit(solution)/shard_map/adamw/pallas_call | solution.py:523

commit v2 on v0

v2 whole, which is shorter than its diff:
```python
import functools

import jax
import jax.numpy as jnp
from jax import lax
from jax.experimental import pallas as pl
from jax.experimental.pallas import tpu as pltpu
from jax.sharding import PartitionSpec as P

BLOCK = 256
ROWS = 512
VMEM = 64 * 1024 * 1024 - 65536
F32, BF16 = jnp.float32, jnp.bfloat16


def dot(a, b):
    return jnp.dot(a, b, preferred_element_type=F32)


def sigmoid(x):
    return 0.5 * jnp.tanh(0.5 * x) + 0.5


def inverse_rms(wide):
    return lax.rsqrt(jnp.mean(wide * wide, -1, keepdims=True) + 1e-6)


def normed(h):
    wide = h.astype(F32)
    return (wide * inverse_rms(wide)).astype(BF16)


def row_loop(tokens, body):
    for i in range(tokens // ROWS):
        body(slice(i * ROWS, (i + 1) * ROWS))


def forward_kernel(x, gate, up, down, out, a, total):
    tokens = x.shape[0]
    j = pl.program_id(0)

    @pl.when(j == 0)
    def _():
        def start(rows):
            a[rows, :] = normed(x[rows, :])
            total[rows, :] = jnp.zeros((ROWS, total.shape[1]), F32)

        row_loop(tokens, start)

    def rows_of(rows):
        g = dot(a[rows, :], gate[0])
        u = dot(a[rows, :], up[0])
        hidden = (g * sigmoid(g) * u).astype(BF16)
        total[rows, :] += dot(hidden, down[0])

    row_loop(tokens, rows_of)

    @pl.when(j == pl.num_programs(0) - 1)
    def _():
        def finish(rows):
            out[rows, :] = x[rows, :] + total[rows, :].astype(BF16)

        row_loop(tokens, finish)


def block_specs(layer, d):
    return [
        pl.BlockSpec((1, d, BLOCK), lambda j: (layer, 0, j)),
        pl.BlockSpec((1, d, BLOCK), lambda j: (layer, 0, j)),
        pl.BlockSpec((1, BLOCK, d), lambda j: (layer, j, 0)),
    ]


def forward(x, w_gate, w_up, w_down):
    tokens, d = x.shape
    blocks = w_gate.shape[2] // BLOCK
    whole = pl.BlockSpec((tokens, d), lambda j: (0, 0))
    return pl.pallas_call(
        forward_kernel,
        out_shape=jax.ShapeDtypeStruct((tokens, d), BF16),
        grid=(blocks,),
        in_specs=[whole] + block_specs(0, d),
        out_specs=whole,
        scratch_shapes=[pltpu.VMEM((tokens, d), BF16), pltpu.VMEM((tokens, d), F32)],
        compiler_params=pltpu.CompilerParams(vmem_limit_bytes=VMEM),
        name="forward",
    )(x, w_gate, w_up, w_down)


MESH = pl.DeviceIdType.MESH
LANES = 128
STREAMS = ((0, 2, 5), (2, 2, 9), (4, 3, 15), (7, 3, 21), (10, 2, 25), (12, 2, 28))


def backward_kernel(group, blocks, h1, x, dy, gate, up, down, out, norm_out, *scratch):
    (h, by, a, a_t, by_t, both, hidden, down_t, w_t, total, terms, sib, norm, squares), scratch = scratch[:14], scratch[14:]
    ring, scratch = scratch[: len(STREAMS)], scratch[len(STREAMS) :]
    final, sems = scratch[: len(STREAMS)], scratch[len(STREAMS) :]
    load_sem, sib_send, sib_recv, rs_send, rs_recv, ag_send, ag_recv, pass_send, pass_recv, fin_sem, fin_send, fin_recv, norm_send, norm_recv = sems
    tokens, d = h.shape
    height = terms.shape[2]
    all_blocks = 2 * blocks
    chips = group // 2
    t = pl.program_id(0)
    p = lax.div(t, 2)
    me = lax.axis_index("dp")
    z, c = lax.div(me, 2), lax.rem(me, 2)
    sibling = me + 1 - 2 * c
    ahead = (lax.rem(z + 1, chips) * 2 + c, lax.rem(z + chips - 1, chips) * 2 + c)

    def wrapped(q):
        return lax.rem(q + 2 * chips, chips)

    def remote(src, dst, send, recv, to):
        return pltpu.make_async_remote_copy(
            src_ref=src, dst_ref=dst, send_sem=send, recv_sem=recv, device_id={"dp": to}, device_id_type=MESH
        )

    def outbox(block):
        return all_blocks + lax.rem(block, 2)

    def put(row, value):
        done = 0
        while done < value.shape[0]:
            piece, at = divmod(row + done, height)
            size = min(height - at, value.shape[0] - done)
            mine = c if piece % 2 else 1 - c
            index = mine * p + (1 - mine) * outbox(p)
            terms[index, piece // 2, at : at + size, :] = value[done : done + size, :]
            done += size

    def sib_copy(block):
        return remote(terms.at[outbox(block)], sib.at[block], sib_send.at[block], sib_recv.at[block], sibling)

    def rs_copy(s, way, k):
        return remote(ring[s].at[way, k], ring[s].at[way, k + 1], rs_send.at[s, way, k], rs_recv.at[s, way, k], ahead[way])

    def own_terms(block, q, way):
        lanes = slice(way * LANES, (way + 1) * LANES)
        return terms[block, q, :, lanes].astype(F32) + sib[block, q, :, lanes].astype(F32)

    def rs_chunk(way, k):
        return wrapped(z - 1 - k if way == 0 else z + 1 + k)

    def rs_first(s):
        first, count, _ = STREAMS[s]
        for block in range(first, first + count):
            sib_copy(block).wait_recv()
        for way in range(2):
            for i in range(count):
                ring[s][way, 0, i] = own_terms(first + i, rs_chunk(way, 0), way).astype(BF16)
            rs_copy(s, way, 0).start()

    def rs_step(s, k):
        first, count, _ = STREAMS[s]
        for way in range(2):
            rs_copy(s, way, k - 1).wait_recv()
            for i in range(count):
                so_far = ring[s][way, k, i].astype(F32)
                ring[s][way, k, i] = (so_far + own_terms(first + i, rs_chunk(way, k), way)).astype(BF16)
            rs_copy(s, way, k).start()

    def rs_last(s):
        first, count, _ = STREAMS[s]
        for way in range(2):
            rs_copy(s, way, chips - 2).wait_recv()
            for i in range(count):
                so_far = ring[s][way, chips - 1, i].astype(F32)
                summed = (so_far + own_terms(first + i, z, way)).astype(BF16)
                final[s][i, :, way * LANES : (way + 1) * LANES] = summed
                wide = summed.astype(F32)
                squares[...] += jnp.sum(wide * wide, 0, keepdims=True)

    def place(s, q, core, way):
        first, count, _ = STREAMS[s]
        return out.at[pl.ds(first, count), q, core, :, pl.ds(way * LANES, LANES)]

    def ag_chunk(way, k):
        return wrapped(z - k if way == 0 else z + k)

    def ag_copy(s, way, k, src=None):
        here = place(s, ag_chunk(way, k), c, way)
        return remote(here if src is None else src, here, ag_send.at[s, way, k], ag_recv.at[s, way, k], ahead[way])

    def pass_copy(s, way, k):
        here = place(s, ag_chunk(way, k), c, way)
        return remote(here, here, pass_send.at[s, way, k - 1], pass_recv.at[s, way, k - 1], sibling)

    def fin_place(s, core):
        first, count, _ = STREAMS[s]
        return out.at[pl.ds(first, count), z, core]

    def fin_copies(s):
        return (
            pltpu.make_async_copy(final[s], fin_place(s, c), fin_sem.at[s]),
            remote(final[s], fin_place(s, c), fin_send.at[s], fin_recv.at[s], sibling),
        )

    def ag_first(s):
        for way in range(2):
            ag_copy(s, way, 0, final[s].at[:, :, pl.ds(way * LANES, LANES)]).start()
        for copy in fin_copies(s):
            copy.start()

    def ag_step(s, k, go_on):
        for way in range(2):
            ag_copy(s, way, k - 1).wait_recv()
            if go_on:
                ag_copy(s, way, k).start()
            pass_copy(s, way, k).start()

    def norm_copy(k):
        return remote(norm.at[me], norm.at[me], norm_send.at[k], norm_recv.at[k], lax.rem(me + k, group))

    def norm_arrival(k):
        place = norm.at[lax.rem(me + group - k, group)]
        return remote(place, place, norm_send.at[k], norm_recv.at[k], sibling)

    def loads(layer_input, by_output=None):
        copies = [pltpu.make_async_copy(layer_input, h, load_sem.at[0])]
        if by_output is not None:
            copies.append(pltpu.make_async_copy(by_output, by, load_sem.at[1]))
        return copies

    def prepare(rows):
        fresh = normed(h[rows, :])
        a[rows, :] = fresh
        a_t[:, rows] = fresh.T
        by_t[:, rows] = by[rows, :].T

    @pl.when(t == 0)
    def _():
        for copy in loads(h1, dy):
            copy.start()
        barrier = pltpu.get_barrier_semaphore()

        def greet(k, _):
            pl.semaphore_signal(barrier, inc=1, device_id={"dp": lax.rem(me + k, group)}, device_id_type=MESH)
            return 0

        lax.fori_loop(1, group, greet, 0)
        squares[...] = jnp.zeros(squares.shape, F32)
        for copy in loads(h1, dy):
            copy.wait()

        def start(rows):
            prepare(rows)
            total[rows, :] = jnp.zeros((ROWS, d), F32)

        row_loop(tokens, start)
        pl.semaphore_wait(barrier, group - 1)

    for s, (_, _, first_slot) in enumerate(STREAMS):
        k = t - first_slot

        @pl.when(k == 0)
        def _(s=s):
            rs_first(s)

        @pl.when((k > 0) & (k < chips - 1))
        def _(s=s, k=k):
            rs_step(s, k)

        @pl.when(k == chips - 1)
        def _(s=s):
            rs_last(s)
            ag_first(s)
            if s == len(STREAMS) - 1:
                norm[me] = jnp.broadcast_to(jnp.sum(squares[...], -1, keepdims=True), norm.shape[1:])

                def send(i, _):
                    norm_copy(i).start()
                    return 0

                lax.fori_loop(1, group, send, 0)

        @pl.when((k > chips - 1) & (k < 2 * chips - 2))
        def _(s=s, k=k):
            ag_step(s, k - (chips - 1), True)

        @pl.when(k == 2 * chips - 2)
        def _(s=s):
            ag_step(s, chips - 1, False)

    @pl.when(t == all_blocks)
    def _():
        def by_input(rows):
            wide = h[rows, :].astype(F32)
            scale = inverse_rms(wide)
            by_a = total[rows, :].astype(BF16).astype(F32)
            by_scale = jnp.sum(by_a * wide, -1, keepdims=True)
            by_h = by_a * scale - wide * (scale * scale * scale * by_scale / d)
            by[rows, :] += by_h.astype(BF16)

        row_loop(tokens, by_input)
        for copy in loads(x):
            copy.start()
            copy.wait()
        row_loop(tokens, prepare)

    @pl.when((t < 2 * all_blocks) & (lax.rem(t, 2) == 0))
    def _():
        down_t[...] = down[0].T

        def rows_of(rows):
            g = dot(a[rows, :], gate[0])
            u = dot(a[rows, :], up[0])
            by_hidden = dot(by[rows, :], down_t[...]).astype(BF16).astype(F32)
            s = sigmoid(g)
            act = g * s
            hidden[rows, :] = (act * u).astype(BF16)
            both[rows, 0:BLOCK] = (by_hidden * u * (s + act * (1.0 - s))).astype(BF16)
            both[rows, BLOCK:] = (by_hidden * act).astype(BF16)

        row_loop(tokens, rows_of)

    @pl.when((t < 2 * all_blocks) & (lax.rem(t, 2) == 1))
    def _():
        @pl.when(p >= 2)
        def _():
            sib_copy(p - 2).wait_send()

        put(0, dot(a_t[...], both[:, 0:BLOCK]).astype(BF16))
        put(d, dot(a_t[...], both[:, BLOCK:]).astype(BF16))
        by_down = dot(by_t[...], hidden[...])
        for i in range(d // BLOCK):
            put(2 * d + i * BLOCK, by_down[i * BLOCK : (i + 1) * BLOCK, :].T.astype(BF16))
        sib_copy(p).start()

        @pl.when(p < blocks)
        def _():
            w_t[0:BLOCK, :] = gate[0].T
            w_t[BLOCK:, :] = up[0].T

            def by_normed(rows):
                total[rows, :] += dot(both[rows, :], w_t[...])

            row_loop(tokens, by_normed)

    @pl.when(t == pl.num_programs(0) - 1)
    def _():
        def wait_norm(k, _):
            norm_copy(k).wait_send()
            norm_arrival(k).wait_recv()
            return 0

        lax.fori_loop(1, group, wait_norm, 0)
        norm_out[...] = jnp.sum(norm[...], 0)
        for block in range(all_blocks - 2, all_blocks):
            sib_copy(block).wait_send()
        for s in range(len(STREAMS)):
            keep, passed = fin_copies(s)
            keep.wait()
            passed.wait_send()
            remote(final[s], fin_place(s, 1 - c), fin_send.at[s], fin_recv.at[s], sibling).wait_recv()

            def wait_rings(k, _, s=s):
                for way in range(2):
                    rs_copy(s, way, k).wait_send()
                    ag_copy(s, way, k).wait_send()
                    pass_copy(s, way, k + 1).wait_send()
                    there = place(s, ag_chunk(way, k + 1), 1 - c, way)
                    remote(there, there, pass_send.at[s, way, k], pass_recv.at[s, way, k], sibling).wait_recv()
                return 0

            lax.fori_loop(0, chips - 1, wait_rings, 0)


def backward(group, h1, x, dy, w_gate, w_up, w_down):
    tokens, d = x.shape
    layers = w_gate.shape[0]
    blocks, chips = w_gate.shape[2] // BLOCK, group // 2
    height = 3 * d // group
    steps = chips - 1

    def layer_block(t):
        p = jnp.minimum(lax.div(t, 2), layers * blocks - 1)
        return layers - 1 - lax.div(p, blocks), lax.rem(p, blocks)

    def tall(t):
        layer, j = layer_block(t)
        return layer, 0, j

    def flat(t):
        layer, j = layer_block(t)
        return layer, j, 0

    anywhere = pl.BlockSpec(memory_space=pl.ANY)
    dma = pltpu.SemaphoreType.DMA
    rows = pltpu.VMEM((tokens, d), BF16)
    columns = pltpu.VMEM((d, tokens), BF16)
    ring_sems = [dma((len(STREAMS), 2, steps))] * 6
    return pl.pallas_call(
        functools.partial(backward_kernel, group, blocks),
        out_shape=[
            jax.ShapeDtypeStruct((layers * blocks, chips, 2, height, BLOCK), BF16),
            jax.ShapeDtypeStruct((8, LANES), F32),
        ],
        grid=(STREAMS[-1][2] + 2 * steps + 1,),
        in_specs=[anywhere] * 3
        + [pl.BlockSpec((1, d, BLOCK), tall), pl.BlockSpec((1, d, BLOCK), tall), pl.BlockSpec((1, BLOCK, d), flat)],
        out_specs=[anywhere, pl.BlockSpec((8, LANES), lambda t: (0, 0))],
        scratch_shapes=[
            rows,
            rows,
            rows,
            columns,
            columns,
            pltpu.VMEM((tokens, 2 * BLOCK), BF16),
            pltpu.VMEM((tokens, BLOCK), BF16),
            pltpu.VMEM((d, BLOCK), BF16),
            pltpu.VMEM((2 * BLOCK, d), BF16),
            pltpu.VMEM((tokens, d), F32),
            pltpu.VMEM((layers * blocks + 2, chips, height, BLOCK), BF16),
            pltpu.VMEM((layers * blocks, chips, height, BLOCK), BF16),
            pltpu.VMEM((group, 8, LANES), F32),
            pltpu.VMEM((1, LANES), F32),
            *[pltpu.VMEM((2, chips, count, height, LANES), BF16) for _, count, _ in STREAMS],
            *[pltpu.VMEM((count, height, BLOCK), BF16) for _, count, _ in STREAMS],
            dma((2,)),
            dma((layers * blocks,)),
            dma((layers * blocks,)),
            *ring_sems,
            *[dma((len(STREAMS),))] * 3,
            dma((group,)),
            dma((group,)),
        ],
        compiler_params=pltpu.CompilerParams(vmem_limit_bytes=VMEM, collective_id=0, has_side_effects=True),
        name="backward",
    )(h1, x, dy, w_gate, w_up, w_down)


def adamw_kernel(parts, d, factor, g, *refs):
    ws, ms, vs, new_ws, new_ms, new_vs = (refs[i : i + 3] for i in range(0, 18, 3))
    f = factor[0]

    def update(i, at, grad):
        grad = grad.astype(F32) * f
        m = 0.9 * ms[i][at] + 0.1 * grad
        v = 0.95 * vs[i][at] + 0.05 * grad * grad
        w = ws[i][at].astype(F32)
        new_ws[i][at] = (w - 0.02 * (m * lax.rsqrt(v + 1e-8) + 0.1 * w)).astype(BF16)
        new_ms[i][at] = m
        new_vs[i][at] = v

    def grad_rows(start):
        return g[0, start : start + BLOCK, :]

    for i in range(2):
        for t in range(d // BLOCK):
            update(i, (0, slice(t * BLOCK, (t + 1) * BLOCK), slice(None)), grad_rows(i * d + t * BLOCK))
    for t in range(d // BLOCK):
        update(2, (0, slice(None), slice(t * BLOCK, (t + 1) * BLOCK)), grad_rows(2 * d + t * BLOCK))


def adamw(factor, g, weights, m, v):
    layers, d, ff = weights[0].shape
    blocks = ff // BLOCK
    tall = pl.BlockSpec((1, d, BLOCK), lambda l, j: (l, 0, j))
    flat = pl.BlockSpec((1, BLOCK, d), lambda l, j: (l, j, 0))
    three = [tall, tall, flat]
    return pl.pallas_call(
        functools.partial(adamw_kernel, 1, d),
        out_shape=[jax.ShapeDtypeStruct(o.shape, o.dtype) for o in (*weights, *m, *v)],
        grid=(layers, blocks),
        in_specs=[pl.BlockSpec(memory_space=pltpu.SMEM), pl.BlockSpec((1, 3 * d, BLOCK), lambda l, j: ((layers - 1 - l) * blocks + j, 0, 0))] + three * 3,
        out_specs=three * 3,
        compiler_params=pltpu.CompilerParams(vmem_limit_bytes=VMEM),
        name="adamw",
    )(factor, g, *weights, *m, *v)


def solution(mesh):
    group = mesh.shape["dp"]

    def step(x, dy, *arrays):
        weights, m, v = (arrays[i : i + 3] for i in (0, 3, 6))
        h1 = forward(x[0], *weights)
        g, squares = backward(group, h1, x[0], dy[0], *weights)
        g = g.reshape(g.shape[0], -1, g.shape[-1])
        factor = jnp.minimum(1.0, 0.5 * lax.rsqrt(squares[0, :1] / g.size + 1e-30))
        return tuple(adamw(factor, g, weights, m, v))

    return jax.shard_map(
        step,
        mesh=mesh,
        in_specs=(P(("rep", "dp"), None, None),) * 2 + (P(None, None, None),) * 9,
        out_specs=(P("rep", None, None),) * 9,
        check_vma=False,
    )
```

time: 497 us -> 326 us (0.66); the launches traced: 490 us -> 326 us
  Pallas kernels: 0 us -> 324 us
  waiting for transfers between devices: 195 us -> 0 us
  matrix products: 187 us -> 0 us
  other arithmetic: 80.7 us -> 0 us
  between operations: 16.8 us -> 1.52 us
  local copies, waits for them, and re-layouts: 9.95 us -> 1.19 us
    pallas_call x0 -> x3, Pallas kernels: none -> 324 us  [the longest x1 237 us: backward(): pl.pallas_call(functools.partial(backward_kernel, group, blocks), out_sha...]
    psum x1 -> x0, waiting for transfers between devices: 195 us -> none  [step(): summed[number] = [lax.psum(by_w[name], 'dp') for name in NAMES]]
    dot_general x15 -> x0, matrix products: 187 us -> none  [the longest x5 71.4 us: layer(): gate = jnp.dot(a, w['w_gate'], preferred_element_type=jnp.float32)]
    convert_element_type x2 -> x0, other arithmetic: 59.2 us -> none  [adamw(): return ((w - 0.02 * step).astype(jnp.bfloat16), m, v)]
    reduce_sum x4 -> x0, other arithmetic: 16.3 us -> none  [the longest x3 15.7 us: step(): jnp.sum(g * g)]
    unnamed x46 -> x0, local copies, waits for them, and re-layouts: 9.95 us -> none
    add_any x1 -> x0, other arithmetic: 5.15 us -> none  [normed(): wide = h.astype(jnp.float32)]
  transfers between devices with their start and end apart: 1 -> 0, of which waited for: 1 -> 0; matrix products, arithmetic and copies ran while one was open for 0% -> 0% of each run, Pallas kernels for 0% -> 0%
where the time goes in v2:
time: 326 us
  Pallas kernels  324 us (99%)
    pallas_call x1, Pallas kernels, backward(): pl.pallas_call(functools.partial(backward_kernel, group, blocks), out_sha...  237 us
    pallas_call x1, Pallas kernels, adamw(): pl.pallas_call(functools.partial(adamw_kernel, 1, d), out_shape=[jax.Shap...  60.3 us
    pallas_call x1, Pallas kernels, forward(): pl.pallas_call(forward_kernel, out_shape=jax.ShapeDtypeStruct((tokens, d)...  26 us

profile of v2, /device:TPU:21, one launch (start us, length us, event | category | flops | bytes accessed | tf_op | source)
XLA Modules:
  0.0 326.3 jit_solution(16294567375082290131)
XLA Ops:
  0.6 26.0 %forward.1.h1 = bf16[2048,768]{1,0:T(8,128)(2,1)} custom-call(bf16[2048,768]{1,0:T(8,128)(2,1)} %bitcast.5, bf16[2,768,1792]{2,1,0:T(8,128)(2,1)} %refs_0_.1, bf16[2,768,1792]{2,1,0:T(8,128)(2,1)} %refs_1_.1, bf16[2,1792,768]{2,1,0:T(8,128)(2,1)} %refs_2_.1), custom_call_target="tpu_custom_call" | custom-call | tf_op jit(solution)/shard_map/forward/pallas_call | solution.py:78
  26.7 237.3 %backward.1 = (bf16[14,8,2,144,256]{4,3,2,1,0:T(8,128)(2,1)}, f32[8,128]{1,0:T(8,128)}) custom-call(bf16[2048,768]{1,0:T(8,128)(2,1)} %forward.1.h1, bf16[2048,768]{1,0:T(8,128)(2,1)} %bitcast.6, bf16[2048,768]{1,0:T(8,128)(2,1)} %bitcast.7, bf16[2,768,1792]{2,1,0:T(8,128)(2,1)} %refs_0_.1, bf16[2,768,1792]{2,1,0:T(8,128)(2,1)} %refs_1_.1, ...), custom_call_target="tpu_custom_call" | custom-call | tf_op jit(solution)/shard_map/backward/pallas_call | solution.py:393
  263.9 1.2 slice.3
  265.8 60.3 %adamw.1 = (bf16[2,768,1792]{2,1,0:T(8,128)(2,1)}, bf16[2,768,1792]{2,1,0:T(8,128)(2,1)}, bf16[2,1792,768]{2,1,0:T(8,128)(2,1)}, f32[2,768,1792]{2,1,0:T(8,128)}...) custom-call(f32[1]{0:T(128)} %bitcast.2.factor, ...), custom_call_target="tpu_custom_call" | custom-call | tf_op jit(solution)/shard_map/adamw/pallas_call | solution.py:462

commit v3 on v2

--- a/solution.py
+++ b/solution.py
@@ -89,7 +89,16 @@
 
 MESH = pl.DeviceIdType.MESH
 LANES = 128
-STREAMS = ((0, 2, 5), (2, 2, 9), (4, 3, 15), (7, 3, 21), (10, 2, 25), (12, 2, 28))
+STREAMS = (
+    (0, 2, 5, 16),
+    (2, 2, 8, 15),
+    (4, 2, 12, 23),
+    (6, 1, 14, 21),
+    (7, 2, 19, 35),
+    (9, 2, 23, 35),
+    (11, 2, 26, 35),
+    (13, 1, 28, 35),
+)
 
 
 def backward_kernel(group, blocks, h1, x, dy, gate, up, down, out, norm_out, *scratch):
@@ -143,7 +152,7 @@
         return wrapped(z - 1 - k if way == 0 else z + 1 + k)
 
     def rs_first(s):
-        first, count, _ = STREAMS[s]
+        first, count = STREAMS[s][:2]
         for block in range(first, first + count):
             sib_copy(block).wait_recv()
         for way in range(2):
@@ -152,7 +161,7 @@
             rs_copy(s, way, 0).start()
 
     def rs_step(s, k):
-        first, count, _ = STREAMS[s]
+        first, count = STREAMS[s][:2]
         for way in range(2):
             rs_copy(s, way, k - 1).wait_recv()
             for i in range(count):
@@ -161,7 +170,7 @@
             rs_copy(s, way, k).start()
 
     def rs_last(s):
-        first, count, _ = STREAMS[s]
+        first, count = STREAMS[s][:2]
         for way in range(2):
             rs_copy(s, way, chips - 2).wait_recv()
             for i in range(count):
@@ -172,7 +181,7 @@
                 squares[...] += jnp.sum(wide * wide, 0, keepdims=True)
 
     def place(s, q, core, way):
-        first, count, _ = STREAMS[s]
+        first, count = STREAMS[s][:2]
         return out.at[pl.ds(first, count), q, core, :, pl.ds(way * LANES, LANES)]
 
     def ag_chunk(way, k):
@@ -187,7 +196,7 @@
         return remote(here, here, pass_send.at[s, way, k - 1], pass_recv.at[s, way, k - 1], sibling)
 
     def fin_place(s, core):
-        first, count, _ = STREAMS[s]
+        first, count = STREAMS[s][:2]
         return out.at[pl.ds(first, count), z, core]
 
     def fin_copies(s):
@@ -250,8 +259,8 @@
         row_loop(tokens, start)
         pl.semaphore_wait(barrier, group - 1)
 
-    for s, (_, _, first_slot) in enumerate(STREAMS):
-        k = t - first_slot
+    for s, (_, _, sums_slot, results_slot) in enumerate(STREAMS):
+        k = t - sums_slot
 
         @pl.when(k == 0)
         def _(s=s):
@@ -264,7 +273,6 @@
         @pl.when(k == chips - 1)
         def _(s=s):
             rs_last(s)
-            ag_first(s)
             if s == len(STREAMS) - 1:
                 norm[me] = jnp.broadcast_to(jnp.sum(squares[...], -1, keepdims=True), norm.shape[1:])
 
@@ -274,11 +282,17 @@
 
                 lax.fori_loop(1, group, send, 0)
 
-        @pl.when((k > chips - 1) & (k < 2 * chips - 2))
+        k = t - results_slot
+
+        @pl.when(k == 0)
+        def _(s=s):
+            ag_first(s)
+
+        @pl.when((k > 0) & (k < chips - 1))
         def _(s=s, k=k):
-            ag_step(s, k - (chips - 1), True)
-
-        @pl.when(k == 2 * chips - 2)
+            ag_step(s, k, True)
+
+        @pl.when(k == chips - 1)
         def _(s=s):
             ag_step(s, chips - 1, False)
 
@@ -396,7 +410,7 @@
             jax.ShapeDtypeStruct((layers * blocks, chips, 2, height, BLOCK), BF16),
             jax.ShapeDtypeStruct((8, LANES), F32),
         ],
-        grid=(STREAMS[-1][2] + 2 * steps + 1,),
+        grid=(max(slot for *_, slot in STREAMS) + chips,),
         in_specs=[anywhere] * 3
         + [pl.BlockSpec((1, d, BLOCK), tall), pl.BlockSpec((1, d, BLOCK), tall), pl.BlockSpec((1, BLOCK, d), flat)],
         out_specs=[anywhere, pl.BlockSpec((8, LANES), lambda t: (0, 0))],
@@ -415,8 +429,8 @@
             pltpu.VMEM((layers * blocks, chips, height, BLOCK), BF16),
             pltpu.VMEM((group, 8, LANES), F32),
             pltpu.VMEM((1, LANES), F32),
-            *[pltpu.VMEM((2, chips, count, height, LANES), BF16) for _, count, _ in STREAMS],
-            *[pltpu.VMEM((count, height, BLOCK), BF16) for _, count, _ in STREAMS],
+            *[pltpu.VMEM((2, chips, count, height, LANES), BF16) for _, count, *_ in STREAMS],
+            *[pltpu.VMEM((count, height, BLOCK), BF16) for _, count, *_ in STREAMS],
             dma((2,)),
             dma((layers * blocks,)),
             dma((layers * blocks,)),

time: 326 us -> 325 us (level)
  no operation moved by 1% of the time
where the time goes in v3:
time: 325 us
  Pallas kernels  322 us (99%)
    pallas_call x1, Pallas kernels, backward(): pl.pallas_call(functools.partial(backward_kernel, group, blocks), out_sha...  236 us
    pallas_call x1, Pallas kernels, adamw(): pl.pallas_call(functools.partial(adamw_kernel, 1, d), out_shape=[jax.Shap...  60.3 us
    pallas_call x1, Pallas kernels, forward(): pl.pallas_call(forward_kernel, out_shape=jax.ShapeDtypeStruct((tokens, d)...  26 us

profile of v3, /device:TPU:21, one launch (start us, length us, event | category | flops | bytes accessed | tf_op | source)
XLA Modules:
  0.0 324.9 jit_solution(8929427558098675494)
XLA Ops:
  0.6 26.0 %forward.1.h1 = bf16[2048,768]{1,0:T(8,128)(2,1)} custom-call(bf16[2048,768]{1,0:T(8,128)(2,1)} %bitcast.5, bf16[2,768,1792]{2,1,0:T(8,128)(2,1)} %refs_0_.1, bf16[2,768,1792]{2,1,0:T(8,128)(2,1)} %refs_1_.1, bf16[2,1792,768]{2,1,0:T(8,128)(2,1)} %refs_2_.1), custom_call_target="tpu_custom_call" | custom-call | tf_op jit(solution)/shard_map/forward/pallas_call | solution.py:78
  26.7 235.9 %backward.1 = (bf16[14,8,2,144,256]{4,3,2,1,0:T(8,128)(2,1)}, f32[8,128]{1,0:T(8,128)}) custom-call(bf16[2048,768]{1,0:T(8,128)(2,1)} %forward.1.h1, bf16[2048,768]{1,0:T(8,128)(2,1)} %bitcast.6, bf16[2048,768]{1,0:T(8,128)(2,1)} %bitcast.7, bf16[2,768,1792]{2,1,0:T(8,128)(2,1)} %refs_0_.1, bf16[2,768,1792]{2,1,0:T(8,128)(2,1)} %refs_1_.1, ...), custom_call_target="tpu_custom_call" | custom-call | tf_op jit(solution)/shard_map/backward/pallas_call | solution.py:407
  262.6 1.2 slice.3
  264.5 60.3 %adamw.1 = (bf16[2,768,1792]{2,1,0:T(8,128)(2,1)}, bf16[2,768,1792]{2,1,0:T(8,128)(2,1)}, bf16[2,1792,768]{2,1,0:T(8,128)(2,1)}, f32[2,768,1792]{2,1,0:T(8,128)}...) custom-call(f32[1]{0:T(128)} %bitcast.2.factor, ...), custom_call_target="tpu_custom_call" | custom-call | tf_op jit(solution)/shard_map/adamw/pallas_call | solution.py:476
